TPU v7x, 128 devices: a whole 4x4x4 slice. The times are simulated.
128 devices in a mesh: grp: 4 (over y), tile: 32 (over x, z, core).
Axes of the slice: x: 4, y: 4, z: 4, core: 2. Of those that a mesh axis runs over, the one named last changes fastest.
Arguments:
- base_rhs: float32 [1024, 16384], P('grp', 'tile'), may hold values from -6 to 6
- depth: float32 [1024, 16384], P('grp', 'tile'), may hold values from 0.25 to 2
- ssh_prev: float32 [1024, 16384], P('grp', 'tile'), may hold values from -6 to 6
- currents: float32 [2, 1024, 16384], P(None, 'grp', 'tile'), may hold values from -3 to 3
- land_blocks: int32 [128, 2048], P('grp', 'tile'), may hold values 0 or 1
- ice_thick: float32 [2, 256, 16384], P(None, 'grp', 'tile'), may hold values from 0.25 to 4
- ice_blocks: int32 [2, 32, 2048], P(None, 'grp', 'tile'), may hold values 0 or 1
- ice_vel: float32 [2, 2, 256, 16384], P(None, None, 'grp', 'tile'), may hold values from -3 to 3
- ice_stress: float32 [3, 2, 256, 16384], P(None, None, 'grp', 'tile'), may hold values from -5 to 5
- wind: float32 [2, 2, 256, 16384], P(None, None, 'grp', 'tile'), may hold values from -6 to 6
Outputs:
- ssh: float32 [1024, 16384], P('grp', 'tile')
- ice_vel_out: float32 [2, 2, 256, 16384], P(None, None, 'grp', 'tile')
- ice_stress_out: float32 [3, 2, 256, 16384], P(None, None, 'grp', 'tile')
All inputs are finite; a program needn't handle non-finite values. No bound on the sum of `land_blocks` or of `ice_blocks` on one device may be relied on, other than what follows from the above.
Results may differ from a plain program's by a relative error of at most 0.0001.
Values sent between devices are 32-bit elements; how exact they have to be, the bound alone decides.
A program may use at most 64 MiB of HBM per device.

v0:
```python
import jax
import jax.numpy as jnp
from jax import lax
from jax.sharding import Mesh
from jax.sharding import PartitionSpec as P

BS = 8
NSUB = 8
ITERS = 3
GRP_TILE = ("grp", "tile_0", "tile_1", "tile_2")
TILE = ("tile_0", "tile_1", "tile_2")
DAMP = 0.05
RELAX = 0.2
STRENGTH = 0.5
DRAG = 1.0
STEP = 0.5


def with_halo(array, sides, width):
    edges = {}
    for axis, dim in sides:
        devices, length = (lax.axis_size(axis), array.shape[dim])
        up = [(i, (i + 1) % devices) for i in range(devices - 1)]
        last = lax.slice_in_dim(array, length - width, length, axis=dim)
        first = lax.slice_in_dim(array, 0, width, axis=dim)
        edges[dim] = (
            lax.ppermute(last, axis, up),
            lax.ppermute(first, axis, [(b, a) for a, b in up]),
        )
    done = []
    for _, dim in sides:
        low, high = edges[dim]
        around = [(width, width) if d in done else (0, 0) for d in range(array.ndim)]
        array = jnp.concatenate([jnp.pad(low, around), array, jnp.pad(high, around)], axis=dim)
        done.append(dim)
    return array


def by_axis(array, axes):
    for axis in axes:
        array = lax.psum(array, axis)
    return array


def extended(array, sides, width):
    for axis, dim in sides:
        devices, length = (lax.axis_size(axis), array.shape[dim])
        up = [(i, (i + 1) % devices) for i in range(devices - 1)]
        down = [(j, i) for i, j in up]
        last = lax.slice_in_dim(array, length - width, length, axis=dim)
        first = lax.slice_in_dim(array, 0, width, axis=dim)
        before = lax.ppermute(last, axis, up)
        after = lax.ppermute(first, axis, down)
        array = jnp.concatenate([before, array, after], axis=dim)
    return array


def strain_rates(u_pad, v_pad):
    du_dx = u_pad[..., 1:, :-1] - u_pad[..., :-1, :-1]
    du_dy = u_pad[..., :-1, 1:] - u_pad[..., :-1, :-1]
    dv_dx = v_pad[..., 1:, :-1] - v_pad[..., :-1, :-1]
    dv_dy = v_pad[..., :-1, 1:] - v_pad[..., :-1, :-1]
    return (du_dx + dv_dy, du_dx - dv_dy, du_dy + dv_dx)


def relax_stress(previous, strength, div_rate, tens_rate, shear_rate):
    deformation = jnp.sqrt(
        div_rate * div_rate + tens_rate * tens_rate + shear_rate * shear_rate + 1.0
    )
    relax_scale = 1.0 / (1.0 + RELAX)
    div_part = (previous[0] + RELAX * strength * (div_rate / deformation - 1.0)) * relax_scale
    tens_part = (previous[1] + RELAX * strength * tens_rate / deformation) * relax_scale
    shear_part = (previous[2] + RELAX * strength * shear_rate / deformation) * relax_scale
    return jnp.stack([div_part, tens_part, shear_part])


def along_rows(field):
    return field[..., 1:, 1:] - field[..., :-1, 1:]


def along_cols(field):
    return field[..., 1:, 1:] - field[..., 1:, :-1]


def stress_force(stress_pad):
    force_x = 0.5 * along_rows(stress_pad[0] + stress_pad[1]) + along_cols(stress_pad[2])
    force_y = 0.5 * along_cols(stress_pad[0] - stress_pad[1]) + along_rows(stress_pad[2])
    return jnp.stack([force_x, force_y])


def momentum(velocity, force, ice_mass, ice_cover, wind, ocean_flow):
    return (
        ice_cover
        * (ice_mass * velocity + STEP * (force + wind + DRAG * ocean_flow))
        / (ice_mass + STEP * DRAG)
    )


def face_weights(depth_pad):
    centre = depth_pad[1:-1, 1:-1]
    return (
        centre * depth_pad[2:, 1:-1],
        centre * depth_pad[:-2, 1:-1],
        centre * depth_pad[1:-1, 2:],
        centre * depth_pad[1:-1, :-2],
    )


def apply_operator(field_pad, weights):
    field = field_pad[1:-1, 1:-1]
    north_weight, south_weight, east_weight, west_weight = weights
    return (
        DAMP * field
        + north_weight * (field - field_pad[2:, 1:-1])
        + south_weight * (field - field_pad[:-2, 1:-1])
        + east_weight * (field - field_pad[1:-1, 2:])
        + west_weight * (field - field_pad[1:-1, :-2])
    )


def expand(blocks):
    return jnp.repeat(jnp.repeat(blocks, BS, axis=-2), BS, axis=-1).astype(jnp.float32)


def operate(field, weights):
    field_pad = with_halo(field, (("grp", 0), (TILE, 1)), 1)
    return apply_operator(field_pad, weights)


def pair_sums(residual, precond, applied):
    return (
        by_axis(jnp.sum(residual * precond), GRP_TILE),
        by_axis(jnp.sum(precond * applied), GRP_TILE),
    )


def local_subcycle(velocity, stress, strength, ice_mass, ice_cover, wind, ocean_flow):
    vel_pad = jnp.pad(velocity, ((0, 0), (0, 0), (1, 1), (1, 1)))
    strain = strain_rates(vel_pad[0], vel_pad[1])
    stress = relax_stress(
        stress, strength, strain[0][:, 1:, 1:], strain[1][:, 1:, 1:], strain[2][:, 1:, 1:]
    )
    stress_pad = jnp.pad(stress, ((0, 0), (0, 0), (1, 0), (1, 0)))
    velocity = momentum(velocity, stress_force(stress_pad), ice_mass, ice_cover, wind, ocean_flow)
    return (velocity, stress)


def shards(
    base_rhs,
    depth,
    ssh_prev,
    currents,
    land_blocks,
    ice_thick,
    ice_blocks,
    ice_vel,
    ice_stress,
    wind,
):
    groups = lax.axis_size("grp")
    grp_index = lax.axis_index("grp")
    ocean_cols = base_rhs.shape[1]
    ice_rows = ice_thick.shape[1]
    cap_rows = ice_rows * groups
    wet_cells = expand(land_blocks)
    ice_cover = expand(ice_blocks)
    at_north = (grp_index == 0).astype(jnp.float32)
    at_south = (grp_index == groups - 1).astype(jnp.float32)
    outgoing = jnp.stack([currents * at_north, currents * at_south], axis=1)
    outgoing = outgoing.reshape(2, 2, groups, ice_rows, ocean_cols)
    incoming = lax.all_to_all(outgoing, "grp", split_axis=2, concat_axis=2, tiled=True)
    ocean_flow = jnp.sum(incoming, axis=2)
    strength = STRENGTH * ice_thick * ice_cover
    ice_mass = ice_thick * ice_cover + 1.0
    velocity = ice_vel
    stress = ice_stress
    bundle = jnp.concatenate(
        [velocity, stress, wind, ocean_flow, strength[None], ice_mass[None], ice_cover[None]],
        axis=0,
    )
    widened = extended(bundle, (("grp", 2), (TILE, 3)), NSUB)
    wide_vel = widened[0:2]
    wide_stress = widened[2:5]
    wide_wind = widened[5:7]
    wide_flow = widened[7:9]
    wide_strength = widened[9]
    wide_mass = widened[10]
    wide_cover = widened[11]
    for subcycle in range(NSUB):
        wide_vel, wide_stress = local_subcycle(
            wide_vel, wide_stress, wide_strength, wide_mass, wide_cover, wide_wind, wide_flow
        )
    velocity = wide_vel[:, :, NSUB : NSUB + ice_rows, NSUB : NSUB + ocean_cols]
    stress = wide_stress[:, :, NSUB : NSUB + ice_rows, NSUB : NSUB + ocean_cols]
    ice_drag = DRAG * ice_cover * (velocity - ocean_flow)
    empty_slot = jnp.zeros_like(ice_drag[:, 0])
    parcel = jnp.stack([ice_drag[:, 0]] + [empty_slot] * (groups - 2) + [ice_drag[:, 1]], axis=1)
    returned = lax.all_to_all(parcel, "grp", split_axis=1, concat_axis=1, tiled=True).reshape(
        2, cap_rows, ocean_cols
    )
    ocean_drag = jnp.where(
        grp_index == 0, returned, jnp.where(grp_index == groups - 1, returned, 0.0)
    )
    forcing_pad = with_halo(
        jnp.stack([ocean_drag[0], ocean_drag[1], depth * wet_cells]), (("grp", 1), (TILE, 2)), 1
    )
    spread = (
        forcing_pad[0, 1:-1, 1:-1]
        - forcing_pad[0, :-2, 1:-1]
        + (forcing_pad[1, 1:-1, 1:-1] - forcing_pad[1, 1:-1, :-2])
    )
    forcing = wet_cells * (base_rhs + spread)
    weights = face_weights(forcing_pad[2])
    diagonal = DAMP + weights[0] + weights[1] + weights[2] + weights[3]
    solution = ssh_prev
    residual = forcing - operate(solution, weights)
    precond = residual / diagonal
    applied = operate(precond, weights)
    precond_norm, curvature_sum = pair_sums(residual, precond, applied)
    step_size = precond_norm / curvature_sum
    direction = precond
    search_image = applied
    for iteration in range(ITERS):
        solution = solution + step_size * direction
        residual = residual - step_size * search_image
        if iteration + 1 < ITERS:
            precond = residual / diagonal
            applied = operate(precond, weights)
            norm_next, curvature_sum = pair_sums(residual, precond, applied)
            beta_ratio = norm_next / precond_norm
            step_size = norm_next / (curvature_sum - beta_ratio * norm_next / step_size)
            direction = precond + beta_ratio * direction
            search_image = applied + beta_ratio * search_image
            precond_norm = norm_next
    return (solution, velocity, stress)


def solution(mesh):
    finer = Mesh(
        mesh.devices.reshape(mesh.shape["grp"], 4, 4, 2), ("grp", "tile_0", "tile_1", "tile_2")
    )
    return jax.shard_map(
        shards,
        mesh=finer,
        in_specs=(
            P("grp", TILE),
            P("grp", TILE),
            P("grp", TILE),
            P(None, "grp", TILE),
            P("grp", TILE),
            P(None, "grp", TILE),
            P(None, "grp", TILE),
            P(None, None, "grp", TILE),
            P(None, None, "grp", TILE),
            P(None, None, "grp", TILE),
        ),
        out_specs=(P("grp", TILE), P(None, None, "grp", TILE), P(None, None, "grp", TILE)),
        check_vma=False,
    )
```

profile of v0, /device:TPU:1, one launch (start us, length us, event | category | flops | bytes accessed | tf_op | source)
XLA Modules:
  0.0 336.6 jit_solution(16348324338508460184)
XLA Ops:
  3.9 5.1 %all-to-all-start = ((f32[2,2,4,64,512]{4,3,0,1,2:T(8,128)}), f32[2,2,4,64,512]{4,3,0,1,2:T(8,128)}, u32[]{:S(2)}, u32[]{:S(2)}) async-start(f32[2,2,4,64,512]{4,3,0,1,2:T(8,128)} %copy.115), calls=%async_computation | async-start | bytes 4194304 | tf_op jit(solution)/shard_map/all_to_all | solution.py:171
  12.7 22.3 %all-to-all-done = f32[2,2,4,64,512]{4,3,0,1,2:T(8,128)} async-done(((f32[2,2,4,64,512]{4,3,0,1,2:T(8,128)}), f32[2,2,4,64,512]{4,3,0,1,2:T(8,128)}, u32[]{:S(2)}, u32[]{:S(2)}) %all-to-all-start) | async-done | bytes 2097184 | tf_op jit(solution)/shard_map/all_to_all | solution.py:171
  43.7 5.6 %collective-permute-done = f32[12,2,8,512]{3,2,1,0:T(8,128)S(1)} collective-permute-done((f32[12,2,8,512]{3,2,1,0:T(8,128)S(1)}, f32[12,2,8,512]{3,2,1,0:T(8,128)S(1)}, u32[]{:S(2)}, u32[]{:S(2)}) %collective-permute-start) | collective-permute-done | bytes 393248 | tf_op jit(solution)/shard_map/ppermute | solution.py:52
  49.3 3.9 %collective-permute-done.1 = f32[12,2,8,512]{3,2,1,0:T(8,128)S(1)} collective-permute-done((f32[12,2,8,512]{3,2,1,0:T(8,128)S(1)}, f32[12,2,8,512]{3,2,1,0:T(8,128)S(1)}, u32[]{:S(2)}, u32[]{:S(2)}) %collective-permute-start.1) | collective-permute-done | bytes 393248 | tf_op jit(solution)/shard_map/ppermute | solution.py:53
  57.7 6.1 %collective-permute-start.2 = (f32[12,2,80,8]{2,3,1,0:T(8,128)}, f32[12,2,80,8]{2,3,1,0:T(8,128)}, u32[]{:S(2)}, u32[]{:S(2)}) collective-permute-start(f32[12,2,80,8]{2,3,1,0:T(8,128)} %copy.121), channel_id=1, source_target_pairs={{0,1},{1,2},{2,3},{3,4},{4,5},{5,6},{6,7},{7,8},{8,9},{9,10},{10,1... | collective-permute-start | bytes 184328 | tf_op jit(solution)/shard_map/ppermute | solution.py:52
  74.3 4.6 %pad_maximum_fusion = f32[12,2,80,528]{3,2,1,0:T(8,128)S(1)} fusion(f32[12,2,80,8]{3,2,1,0:T(8,128)} %copy.124, f32[12,2,8,512]{3,2,1,0:T(8,128)} %copy-done.2, f32[12,2,64,512]{3,2,1,0:T(8,128)S(1)} %constant_dynamic-update-slice_fusion, f32[12,2,8,512]{3,2,1,0:T(8,128)S(1)} %collective-permute-done, f32[12,2,80,8]{3,2,1,0:T(8,128)} %copy.123), kind=kLoop, calls=%fused_computation | loop fusion | flops 4055040 | bytes 8110080 | tf_op jit(solution)/shard_map/concatenate | solution.py:54
  112.5 3.6 %all-to-all-start.1 = ((f32[2,4,64,512]{3,2,0,1:T(8,128)}), f32[2,4,64,512]{3,2,0,1:T(8,128)S(1)}, u32[]{:S(2)}, u32[]{:S(2)}) async-start(f32[2,4,64,512]{3,2,0,1:T(8,128)} %pad_maximum_fusion.3), calls=%async_computation.1 | async-start | bytes 2097152 | tf_op jit(solution)/shard_map/all_to_all | solution.py:198
  121.5 7.6 %all-to-all-done.1 = f32[2,4,64,512]{3,2,0,1:T(8,128)S(1)} async-done(((f32[2,4,64,512]{3,2,0,1:T(8,128)}), f32[2,4,64,512]{3,2,0,1:T(8,128)S(1)}, u32[]{:S(2)}, u32[]{:S(2)}) %all-to-all-start.1) | async-done | bytes 1048608 | tf_op jit(solution)/shard_map/all_to_all | solution.py:198
  141.9 4.4 %collective-permute-start.5 = (f32[3,256,1]{1,2,0:T(1,128)S(1)}, f32[3,256,1]{1,2,0:T(1,128)S(1)}, u32[]{:S(2)}, u32[]{:S(2)}) collective-permute-start(f32[3,256,1]{1,2,0:T(1,128)S(1)} %get-tuple-element.96), channel_id=1, source_target_pairs={{0,1},{1,2},{2,3},{3,4},{4,5},{5,6},{6,7},{7,8},{8,9},{9,10},{10,1... | collective-permute-start | bytes 9224 | tf_op jit(solution)/shard_map/ppermute | solution.py:27
  151.6 3.6 %collective-permute-start.11 = (f32[256,1]{0,1:T(1,128)S(1)}, f32[256,1]{0,1:T(1,128)S(1)}, u32[]{:S(2)}, u32[]{:S(2)}) collective-permute-start(f32[256,1]{0,1:T(1,128)S(1)} %get-tuple-element.170), channel_id=1, source_target_pairs={{0,1},{1,2},{2,3},{3,4},{4,5},{5,6},{6,7},{7,8},{8,9},{9,10},{10,1... | collective-permute-start | bytes 3080 | tf_op jit(solution)/shard_map/ppermute | solution.py:27
  157.9 5.6 %collective-permute-start.9 = (f32[1,512]{0,1:T(8,128)}, f32[1,512]{0,1:T(8,128)}, u32[]{:S(2)}, u32[]{:S(2)}) collective-permute-start(f32[1,512]{0,1:T(8,128)} %copy.149), channel_id=1, source_target_pairs={{0,32},{32,64},{64,96},{1,33},{33,65},{65,97},{2,34},{34,66},{66,9... | collective-permute-start | bytes 6152 | tf_op jit(solution)/shard_map/ppermute | solution.py:27
  168.4 3.4 fusion.196
  173.2 4.5 %collective-permute-start.13 = (f32[1,512]{0,1:T(8,128)S(1)}, f32[1,512]{0,1:T(8,128)S(1)}, u32[]{:S(2)}, u32[]{:S(2)}) collective-permute-start(f32[1,512]{0,1:T(8,128)S(1)} %get-tuple-element.165), channel_id=1, source_target_pairs={{0,32},{32,64},{64,96},{1,33},{33,65},{65,97},{2,34},{34,66},{66,9... | collective-permute-start | bytes 6152 | tf_op jit(solution)/shard_map/ppermute | solution.py:27
  179.8 3.7 %collective-permute-start.15 = (f32[256,1]{0,1:T(1,128)S(1)}, f32[256,1]{0,1:T(1,128)S(1)}, u32[]{:S(2)}, u32[]{:S(2)}) collective-permute-start(f32[256,1]{0,1:T(1,128)S(1)} %get-tuple-element.164), channel_id=1, source_target_pairs={{0,1},{1,2},{2,3},{3,4},{4,5},{5,6},{6,7},{7,8},{8,9},{9,10},{10,1... | collective-permute-start | bytes 3080 | tf_op jit(solution)/shard_map/ppermute | solution.py:27
  185.6 9.8 %all-reduce.34 = (f32[]{:T(128)}, f32[]{:T(128)}) all-reduce(f32[]{:T(128)} %get-tuple-element.20, f32[]{:T(128)} %get-tuple-element.19), channel_id=1, replica_groups=mesh['grp'=4,'tile_0'=4,'tile_1'=4,'tile_2'=2] {'grp'}, use_global_device_ids=true, to_apply=%region_2.3 | all-reduce | flops 2 | bytes 16 | tf_op jit(solution)/shard_map/psum | solution.py:41
  195.4 10.2 %all-reduce.31 = (f32[]{:T(128)}, f32[]{:T(128)}) all-reduce(f32[]{:T(128)} %get-tuple-element.37, f32[]{:T(128)} %get-tuple-element.38), channel_id=1, replica_groups=mesh['grp'=4,'tile_0'=4,'tile_1'=4,'tile_2'=2] {'tile_0'}, use_global_device_ids=true, to_apply=%region_3.4 | all-reduce | flops 2 | bytes 16 | tf_op jit(solution)/shard_map/psum | solution.py:41
  205.6 9.1 %all-reduce.28 = (f32[]{:T(128)}, f32[]{:T(128)}) all-reduce(f32[]{:T(128)} %get-tuple-element.31, f32[]{:T(128)} %get-tuple-element.32), channel_id=1, replica_groups=mesh['grp'=4,'tile_0'=4,'tile_1'=4,'tile_2'=2] {'tile_1'}, use_global_device_ids=true, to_apply=%region_4.5 | all-reduce | flops 2 | bytes 16 | tf_op jit(solution)/shard_map/psum | solution.py:41
  214.7 10.6 %all-reduce.37 = (f32[]{:T(128)}, f32[]{:T(128)}) all-reduce(f32[]{:T(128)} %get-tuple-element.25, f32[]{:T(128)} %get-tuple-element.26), channel_id=1, replica_groups=mesh['grp'=4,'tile_0'=4,'tile_1'=4,'tile_2'=2] {'tile_2'}, use_global_device_ids=true, to_apply=%region_5.6 | all-reduce | flops 2 | bytes 16 | tf_op jit(solution)/shard_map/psum | solution.py:41
  229.3 4.0 %collective-permute-start.17 = (f32[1,512]{0,1:T(8,128)S(1)}, f32[1,512]{0,1:T(8,128)S(1)}, u32[]{:S(2)}, u32[]{:S(2)}) collective-permute-start(f32[1,512]{0,1:T(8,128)S(1)} %get-tuple-element.161), channel_id=1, source_target_pairs={{0,32},{32,64},{64,96},{1,33},{33,65},{65,97},{2,34},{34,66},{66,9... | collective-permute-start | bytes 6152 | tf_op jit(solution)/shard_map/ppermute | solution.py:27
  233.3 2.8 collective-permute-start.18
  236.1 3.5 %collective-permute-start.19 = (f32[256,1]{0,1:T(1,128)S(1)}, f32[256,1]{0,1:T(1,128)S(1)}, u32[]{:S(2)}, u32[]{:S(2)}) collective-permute-start(f32[256,1]{0,1:T(1,128)S(1)} %get-tuple-element.160), channel_id=1, source_target_pairs={{0,1},{1,2},{2,3},{3,4},{4,5},{5,6},{6,7},{7,8},{8,9},{9,10},{10,1... | collective-permute-start | bytes 3080 | tf_op jit(solution)/shard_map/ppermute | solution.py:27
  242.5 7.5 %all-reduce.33 = (f32[]{:T(128)}, f32[]{:T(128)}) all-reduce(f32[]{:T(128)} %get-tuple-element.18, f32[]{:T(128)} %get-tuple-element.17), channel_id=1, replica_groups=mesh['grp'=4,'tile_0'=4,'tile_1'=4,'tile_2'=2] {'grp'}, use_global_device_ids=true, to_apply=%region_12.13 | all-reduce | flops 2 | bytes 16 | tf_op jit(solution)/shard_map/psum | solution.py:41
  250.0 7.4 %all-reduce.30 = (f32[]{:T(128)}, f32[]{:T(128)}) all-reduce(f32[]{:T(128)} %get-tuple-element.35, f32[]{:T(128)} %get-tuple-element.36), channel_id=1, replica_groups=mesh['grp'=4,'tile_0'=4,'tile_1'=4,'tile_2'=2] {'tile_0'}, use_global_device_ids=true, to_apply=%region_13.14 | all-reduce | flops 2 | bytes 16 | tf_op jit(solution)/shard_map/psum | solution.py:41
  257.4 9.2 %all-reduce.27 = (f32[]{:T(128)}, f32[]{:T(128)}) all-reduce(f32[]{:T(128)} %get-tuple-element.29, f32[]{:T(128)} %get-tuple-element.30), channel_id=1, replica_groups=mesh['grp'=4,'tile_0'=4,'tile_1'=4,'tile_2'=2] {'tile_1'}, use_global_device_ids=true, to_apply=%region_14.15 | all-reduce | flops 2 | bytes 16 | tf_op jit(solution)/shard_map/psum | solution.py:41
  266.6 10.5 %all-reduce.36 = (f32[]{:T(128)}, f32[]{:T(128)}) all-reduce(f32[]{:T(128)} %get-tuple-element.23, f32[]{:T(128)} %get-tuple-element.24), channel_id=1, replica_groups=mesh['grp'=4,'tile_0'=4,'tile_1'=4,'tile_2'=2] {'tile_2'}, use_global_device_ids=true, to_apply=%region_15.16 | all-reduce | flops 2 | bytes 16 | tf_op jit(solution)/shard_map/psum | solution.py:41
  284.6 4.0 %collective-permute-start.21 = (f32[1,512]{0,1:T(8,128)S(1)}, f32[1,512]{0,1:T(8,128)S(1)}, u32[]{:S(2)}, u32[]{:S(2)}) collective-permute-start(f32[1,512]{0,1:T(8,128)S(1)} %get-tuple-element.157), channel_id=1, source_target_pairs={{0,32},{32,64},{64,96},{1,33},{33,65},{65,97},{2,34},{34,66},{66,9... | collective-permute-start | bytes 6152 | tf_op jit(solution)/shard_map/ppermute | solution.py:27
  288.6 2.8 collective-permute-start.22
  291.4 3.5 %collective-permute-start.23 = (f32[256,1]{0,1:T(1,128)S(1)}, f32[256,1]{0,1:T(1,128)S(1)}, u32[]{:S(2)}, u32[]{:S(2)}) collective-permute-start(f32[256,1]{0,1:T(1,128)S(1)} %get-tuple-element.156), channel_id=1, source_target_pairs={{0,1},{1,2},{2,3},{3,4},{4,5},{5,6},{6,7},{7,8},{8,9},{9,10},{10,1... | collective-permute-start | bytes 3080 | tf_op jit(solution)/shard_map/ppermute | solution.py:27
  298.3 7.2 %all-reduce.32 = (f32[]{:T(128)}, f32[]{:T(128)}) all-reduce(f32[]{:T(128)} %get-tuple-element.16, f32[]{:T(128)} %get-tuple-element.15), channel_id=1, replica_groups=mesh['grp'=4,'tile_0'=4,'tile_1'=4,'tile_2'=2] {'grp'}, use_global_device_ids=true, to_apply=%region_22.23 | all-reduce | flops 2 | bytes 16 | tf_op jit(solution)/shard_map/psum | solution.py:41
  305.5 6.7 %all-reduce.29 = (f32[]{:T(128)}, f32[]{:T(128)}) all-reduce(f32[]{:T(128)} %get-tuple-element.33, f32[]{:T(128)} %get-tuple-element.34), channel_id=1, replica_groups=mesh['grp'=4,'tile_0'=4,'tile_1'=4,'tile_2'=2] {'tile_0'}, use_global_device_ids=true, to_apply=%region_23.24 | all-reduce | flops 2 | bytes 16 | tf_op jit(solution)/shard_map/psum | solution.py:41
  312.2 9.8 %all-reduce.26 = (f32[]{:T(128)}, f32[]{:T(128)}) all-reduce(f32[]{:T(128)} %get-tuple-element.27, f32[]{:T(128)} %get-tuple-element.28), channel_id=1, replica_groups=mesh['grp'=4,'tile_0'=4,'tile_1'=4,'tile_2'=2] {'tile_1'}, use_global_device_ids=true, to_apply=%region_24.25 | all-reduce | flops 2 | bytes 16 | tf_op jit(solution)/shard_map/psum | solution.py:41
  322.0 9.2 %all-reduce.35 = (f32[]{:T(128)}, f32[]{:T(128)}) all-reduce(f32[]{:T(128)} %get-tuple-element.21, f32[]{:T(128)} %get-tuple-element.22), channel_id=1, replica_groups=mesh['grp'=4,'tile_0'=4,'tile_1'=4,'tile_2'=2] {'tile_2'}, use_global_device_ids=true, to_apply=%region_25.26 | all-reduce | flops 2 | bytes 16 | tf_op jit(solution)/shard_map/psum | solution.py:41
  (246 shorter events, 113.0 us)
Async XLA Ops:
  3.9 31.1 %all-to-all-start = ((f32[2,2,4,64,512]{4,3,0,1,2:T(8,128)}), f32[2,2,4,64,512]{4,3,0,1,2:T(8,128)}, u32[]{:S(2)}, u32[]{:S(2)}) async-start(f32[2,2,4,64,512]{4,3,0,1,2:T(8,128)} %copy.115), calls=%async_computation | async-start | bytes 4194304 | tf_op jit(solution)/shard_map/all_to_all | solution.py:171
  9.4 30.4 %copy-start.24 = (f32[2,64,512]{2,1,0:T(8,128)}, f32[2,64,512]{2,1,0:T(8,128)S(1)}, u32[]{:S(2)}) copy-start(f32[2,64,512]{2,1,0:T(8,128)S(1)} %copy.114) | copy-start | bytes 786436
  40.0 9.4 %collective-permute-start = (f32[12,2,8,512]{3,2,1,0:T(8,128)S(1)}, f32[12,2,8,512]{3,2,1,0:T(8,128)S(1)}, u32[]{:S(2)}, u32[]{:S(2)}) collective-permute-start(f32[12,2,8,512]{3,2,1,0:T(8,128)S(1)} %get-tuple-element.93), channel_id=1, source_target_pairs={{0,32},{32,64},{64,96},{1,33},{33,65},{65,97},{2,34},{34,66},{66,9... | collective-permute-start | bytes 1179656 | tf_op jit(solution)/shard_map/ppermute | solution.py:52
  42.4 10.8 %collective-permute-start.1 = (f32[12,2,8,512]{3,2,1,0:T(8,128)S(1)}, f32[12,2,8,512]{3,2,1,0:T(8,128)S(1)}, u32[]{:S(2)}, u32[]{:S(2)}) collective-permute-start(f32[12,2,8,512]{3,2,1,0:T(8,128)S(1)} %get-tuple-element.94), channel_id=1, source_target_pairs={{32,0},{64,32},{96,64},{33,1},{65,33},{97,65},{34,2},{66,34},{98,6... | collective-permute-start | bytes 1179656 | tf_op jit(solution)/shard_map/ppermute | solution.py:53
  57.7 10.2 %collective-permute-start.2 = (f32[12,2,80,8]{2,3,1,0:T(8,128)}, f32[12,2,80,8]{2,3,1,0:T(8,128)}, u32[]{:S(2)}, u32[]{:S(2)}) collective-permute-start(f32[12,2,80,8]{2,3,1,0:T(8,128)} %copy.121), channel_id=1, source_target_pairs={{0,1},{1,2},{2,3},{3,4},{4,5},{5,6},{6,7},{7,8},{8,9},{9,10},{10,1... | collective-permute-start | bytes 184328 | tf_op jit(solution)/shard_map/ppermute | solution.py:52
  65.9 6.2 %collective-permute-start.3 = (f32[12,2,80,8]{2,3,1,0:T(8,128)}, f32[12,2,80,8]{2,3,1,0:T(8,128)}, u32[]{:S(2)}, u32[]{:S(2)}) collective-permute-start(f32[12,2,80,8]{2,3,1,0:T(8,128)} %copy.122), channel_id=1, source_target_pairs={{1,0},{2,1},{3,2},{4,3},{5,4},{6,5},{7,6},{8,7},{9,8},{10,9},{11,1... | collective-permute-start | bytes 184328 | tf_op jit(solution)/shard_map/ppermute | solution.py:53
  112.5 16.7 %all-to-all-start.1 = ((f32[2,4,64,512]{3,2,0,1:T(8,128)}), f32[2,4,64,512]{3,2,0,1:T(8,128)S(1)}, u32[]{:S(2)}, u32[]{:S(2)}) async-start(f32[2,4,64,512]{3,2,0,1:T(8,128)} %pad_maximum_fusion.3), calls=%async_computation.1 | async-start | bytes 2097152 | tf_op jit(solution)/shard_map/all_to_all | solution.py:198
  116.3 14.0 %copy-start.20 = (f32[256,512]{0,1:T(8,128)}, f32[256,512]{0,1:T(8,128)S(1)}, u32[]{:S(2)}) copy-start(f32[256,512]{0,1:T(8,128)S(1)} %copy.157) | copy-start | bytes 1572868
  116.3 49.9 %collective-permute-start.10 = (f32[256,1]{0,1:T(1,128)S(1)}, f32[256,1]{0,1:T(1,128)S(1)}, u32[]{:S(2)}, u32[]{:S(2)}) collective-permute-start(f32[256,1]{0,1:T(1,128)S(1)} %get-tuple-element.169), channel_id=1, source_target_pairs={{1,0},{2,1},{3,2},{4,3},{5,4},{6,5},{7,6},{8,7},{9,8},{10,9},{11,1... | collective-permute-start | bytes 3080 | tf_op jit(solution)/shard_map/ppermute | solution.py:28
  135.5 15.1 %copy-start.32 = (f32[256,512]{1,0:T(8,128)S(1)}, f32[256,512]{1,0:T(8,128)}, u32[]{:S(2)}) copy-start(f32[256,512]{1,0:T(8,128)} %param.10) | copy-start | bytes 1572868
  137.0 18.4 %collective-permute-start.4 = (f32[3,1,512]{2,1,0:T(1,128)S(1)}, f32[3,1,512]{2,1,0:T(1,128)S(1)}, u32[]{:S(2)}, u32[]{:S(2)}) collective-permute-start(f32[3,1,512]{2,1,0:T(1,128)S(1)} %copy.139), channel_id=1, source_target_pairs={{0,32},{32,64},{64,96},{1,33},{33,65},{65,97},{2,34},{34,66},{66,9... | collective-permute-start | bytes 18440 | tf_op jit(solution)/shard_map/ppermute | solution.py:27
  140.5 17.3 %collective-permute-start.6 = (f32[3,1,512]{2,1,0:T(1,128)S(1)}, f32[3,1,512]{2,1,0:T(1,128)S(1)}, u32[]{:S(2)}, u32[]{:S(2)}) collective-permute-start(f32[3,1,512]{2,1,0:T(1,128)S(1)} %copy.141), channel_id=1, source_target_pairs={{32,0},{64,32},{96,64},{33,1},{65,33},{97,65},{34,2},{66,34},{98,6... | collective-permute-start | bytes 18440 | tf_op jit(solution)/shard_map/ppermute | solution.py:28
  141.9 9.8 %collective-permute-start.5 = (f32[3,256,1]{1,2,0:T(1,128)S(1)}, f32[3,256,1]{1,2,0:T(1,128)S(1)}, u32[]{:S(2)}, u32[]{:S(2)}) collective-permute-start(f32[3,256,1]{1,2,0:T(1,128)S(1)} %get-tuple-element.96), channel_id=1, source_target_pairs={{0,1},{1,2},{2,3},{3,4},{4,5},{5,6},{6,7},{7,8},{8,9},{9,10},{10,1... | collective-permute-start | bytes 9224 | tf_op jit(solution)/shard_map/ppermute | solution.py:27
  146.2 18.4 %collective-permute-start.7 = (f32[3,256,1]{1,2,0:T(1,128)S(1)}, f32[3,256,1]{1,2,0:T(1,128)S(1)}, u32[]{:S(2)}, u32[]{:S(2)}) collective-permute-start(f32[3,256,1]{1,2,0:T(1,128)S(1)} %get-tuple-element.95), channel_id=1, source_target_pairs={{1,0},{2,1},{3,2},{4,3},{5,4},{6,5},{7,6},{8,7},{9,8},{10,9},{11,1... | collective-permute-start | bytes 9224 | tf_op jit(solution)/shard_map/ppermute | solution.py:28
  151.6 14.6 %collective-permute-start.11 = (f32[256,1]{0,1:T(1,128)S(1)}, f32[256,1]{0,1:T(1,128)S(1)}, u32[]{:S(2)}, u32[]{:S(2)}) collective-permute-start(f32[256,1]{0,1:T(1,128)S(1)} %get-tuple-element.170), channel_id=1, source_target_pairs={{0,1},{1,2},{2,3},{3,4},{4,5},{5,6},{6,7},{7,8},{8,9},{9,10},{10,1... | collective-permute-start | bytes 3080 | tf_op jit(solution)/shard_map/ppermute | solution.py:27
  155.4 10.9 %collective-permute-start.8 = (f32[1,512]{0,1:T(8,128)}, f32[1,512]{0,1:T(8,128)S(1)}, u32[]{:S(2)}, u32[]{:S(2)}) collective-permute-start(f32[1,512]{0,1:T(8,128)} %copy.146), channel_id=1, source_target_pairs={{32,0},{64,32},{96,64},{33,1},{65,33},{97,65},{34,2},{66,34},{98,6... | collective-permute-start | bytes 6152 | tf_op jit(solution)/shard_map/ppermute | solution.py:28
  157.9 10.5 %collective-permute-start.9 = (f32[1,512]{0,1:T(8,128)}, f32[1,512]{0,1:T(8,128)}, u32[]{:S(2)}, u32[]{:S(2)}) collective-permute-start(f32[1,512]{0,1:T(8,128)} %copy.149), channel_id=1, source_target_pairs={{0,32},{32,64},{64,96},{1,33},{33,65},{65,97},{2,34},{34,66},{66,9... | collective-permute-start | bytes 6152 | tf_op jit(solution)/shard_map/ppermute | solution.py:27
  171.9 12.4 %collective-permute-start.12 = (f32[1,512]{0,1:T(8,128)S(1)}, f32[1,512]{0,1:T(8,128)S(1)}, u32[]{:S(2)}, u32[]{:S(2)}) collective-permute-start(f32[1,512]{0,1:T(8,128)S(1)} %get-tuple-element.166), channel_id=1, source_target_pairs={{32,0},{64,32},{96,64},{33,1},{65,33},{97,65},{34,2},{66,34},{98,6... | collective-permute-start | bytes 6152 | tf_op jit(solution)/shard_map/ppermute | solution.py:28
  173.2 11.1 %collective-permute-start.13 = (f32[1,512]{0,1:T(8,128)S(1)}, f32[1,512]{0,1:T(8,128)S(1)}, u32[]{:S(2)}, u32[]{:S(2)}) collective-permute-start(f32[1,512]{0,1:T(8,128)S(1)} %get-tuple-element.165), channel_id=1, source_target_pairs={{0,32},{32,64},{64,96},{1,33},{33,65},{65,97},{2,34},{34,66},{66,9... | collective-permute-start | bytes 6152 | tf_op jit(solution)/shard_map/ppermute | solution.py:27
  177.7 5.9 %collective-permute-start.14 = (f32[256,1]{0,1:T(1,128)S(1)}, f32[256,1]{0,1:T(1,128)S(1)}, u32[]{:S(2)}, u32[]{:S(2)}) collective-permute-start(f32[256,1]{0,1:T(1,128)S(1)} %get-tuple-element.163), channel_id=1, source_target_pairs={{1,0},{2,1},{3,2},{4,3},{5,4},{6,5},{7,6},{8,7},{9,8},{10,9},{11,1... | collective-permute-start | bytes 3080 | tf_op jit(solution)/shard_map/ppermute | solution.py:28
  179.8 4.5 %collective-permute-start.15 = (f32[256,1]{0,1:T(1,128)S(1)}, f32[256,1]{0,1:T(1,128)S(1)}, u32[]{:S(2)}, u32[]{:S(2)}) collective-permute-start(f32[256,1]{0,1:T(1,128)S(1)} %get-tuple-element.164), channel_id=1, source_target_pairs={{0,1},{1,2},{2,3},{3,4},{4,5},{5,6},{6,7},{7,8},{8,9},{9,10},{10,1... | collective-permute-start | bytes 3080 | tf_op jit(solution)/shard_map/ppermute | solution.py:27
  228.0 12.4 %collective-permute-start.16 = (f32[1,512]{0,1:T(8,128)S(1)}, f32[1,512]{0,1:T(8,128)S(1)}, u32[]{:S(2)}, u32[]{:S(2)}) collective-permute-start(f32[1,512]{0,1:T(8,128)S(1)} %get-tuple-element.162), channel_id=1, source_target_pairs={{32,0},{64,32},{96,64},{33,1},{65,33},{97,65},{34,2},{66,34},{98,6... | collective-permute-start | bytes 6152 | tf_op jit(solution)/shard_map/ppermute | solution.py:28
  229.3 11.1 %collective-permute-start.17 = (f32[1,512]{0,1:T(8,128)S(1)}, f32[1,512]{0,1:T(8,128)S(1)}, u32[]{:S(2)}, u32[]{:S(2)}) collective-permute-start(f32[1,512]{0,1:T(8,128)S(1)} %get-tuple-element.161), channel_id=1, source_target_pairs={{0,32},{32,64},{64,96},{1,33},{33,65},{65,97},{2,34},{34,66},{66,9... | collective-permute-start | bytes 6152 | tf_op jit(solution)/shard_map/ppermute | solution.py:27
  233.3 6.4 %collective-permute-start.18 = (f32[256,1]{0,1:T(1,128)S(1)}, f32[256,1]{0,1:T(1,128)S(1)}, u32[]{:S(2)}, u32[]{:S(2)}) collective-permute-start(f32[256,1]{0,1:T(1,128)S(1)} %get-tuple-element.159), channel_id=1, source_target_pairs={{1,0},{2,1},{3,2},{4,3},{5,4},{6,5},{7,6},{8,7},{9,8},{10,9},{11,1... | collective-permute-start | bytes 3080 | tf_op jit(solution)/shard_map/ppermute | solution.py:28
  236.1 4.2 %collective-permute-start.19 = (f32[256,1]{0,1:T(1,128)S(1)}, f32[256,1]{0,1:T(1,128)S(1)}, u32[]{:S(2)}, u32[]{:S(2)}) collective-permute-start(f32[256,1]{0,1:T(1,128)S(1)} %get-tuple-element.160), channel_id=1, source_target_pairs={{0,1},{1,2},{2,3},{3,4},{4,5},{5,6},{6,7},{7,8},{8,9},{9,10},{10,1... | collective-permute-start | bytes 3080 | tf_op jit(solution)/shard_map/ppermute | solution.py:27
  283.1 13.9 %copy-start.8 = (f32[256,512]{0,1:T(8,128)S(1)}, f32[256,512]{0,1:T(8,128)}, u32[]{:S(2)}) copy-start(f32[256,512]{0,1:T(8,128)} %copy-done.6) | copy-start | bytes 1572868
  283.1 13.8 %collective-permute-start.20 = (f32[1,512]{0,1:T(8,128)S(1)}, f32[1,512]{0,1:T(8,128)S(1)}, u32[]{:S(2)}, u32[]{:S(2)}) collective-permute-start(f32[1,512]{0,1:T(8,128)S(1)} %get-tuple-element.158), channel_id=1, source_target_pairs={{32,0},{64,32},{96,64},{33,1},{65,33},{97,65},{34,2},{66,34},{98,6... | collective-permute-start | bytes 6152 | tf_op jit(solution)/shard_map/ppermute | solution.py:28
  284.6 12.4 %collective-permute-start.21 = (f32[1,512]{0,1:T(8,128)S(1)}, f32[1,512]{0,1:T(8,128)S(1)}, u32[]{:S(2)}, u32[]{:S(2)}) collective-permute-start(f32[1,512]{0,1:T(8,128)S(1)} %get-tuple-element.157), channel_id=1, source_target_pairs={{0,32},{32,64},{64,96},{1,33},{33,65},{65,97},{2,34},{34,66},{66,9... | collective-permute-start | bytes 6152 | tf_op jit(solution)/shard_map/ppermute | solution.py:27
  288.6 8.3 %collective-permute-start.22 = (f32[256,1]{0,1:T(1,128)S(1)}, f32[256,1]{0,1:T(1,128)S(1)}, u32[]{:S(2)}, u32[]{:S(2)}) collective-permute-start(f32[256,1]{0,1:T(1,128)S(1)} %get-tuple-element.155), channel_id=1, source_target_pairs={{1,0},{2,1},{3,2},{4,3},{5,4},{6,5},{7,6},{8,7},{9,8},{10,9},{11,1... | collective-permute-start | bytes 3080 | tf_op jit(solution)/shard_map/ppermute | solution.py:28
  291.4 5.5 %collective-permute-start.23 = (f32[256,1]{0,1:T(1,128)S(1)}, f32[256,1]{0,1:T(1,128)S(1)}, u32[]{:S(2)}, u32[]{:S(2)}) collective-permute-start(f32[256,1]{0,1:T(1,128)S(1)} %get-tuple-element.156), channel_id=1, source_target_pairs={{0,1},{1,2},{2,3},{3,4},{4,5},{5,6},{6,7},{7,8},{8,9},{9,10},{10,1... | collective-permute-start | bytes 3080 | tf_op jit(solution)/shard_map/ppermute | solution.py:27
  297.0 38.1 %copy-start.5 = (f32[256,512]{0,1:T(8,128)S(1)}, f32[256,512]{0,1:T(8,128)}, u32[]{:S(2)}) copy-start(f32[256,512]{0,1:T(8,128)} %copy-done.4) | copy-start | bytes 1572868
  297.0 38.1 %copy-start.22 = (f32[256,512]{0,1:T(8,128)S(1)}, f32[256,512]{0,1:T(8,128)}, u32[]{:S(2)}) copy-start(f32[256,512]{0,1:T(8,128)} %copy-done.20) | copy-start | bytes 1572868
  (30 other events, 223.3 us)
where the time goes:
time: 342 us; the launch traced here: 337 us
  blocking collectives  107 us (31%)
  starting transfers between devices  77.7 us (23%)
  other arithmetic  56.2 us (16%)
  waiting for transfers between devices  44.4 us (13%)
  local copies, waits for them, and re-layouts  39.4 us (12%)
  between operations  11.7 us (3%)
    psum x12, blocking collectives, by_axis(): array = lax.psum(array, axis)  107 us
    ppermute x10, starting transfers between devices, with_halo(): lax.ppermute(last, axis, up)  39 us
    all_to_all x1, waiting for transfers between devices, shards(): lax.all_to_all(outgoing, 'grp', split_axis=2, concat_axis=2, tiled=True)  22.3 us
    ppermute x10, starting transfers between devices, with_halo(): lax.ppermute(first, axis, [(b, a) for a, b in up])  18.2 us
    unnamed x81, local copies, waits for them, and re-layouts  12.2 us
    ppermute x2, starting transfers between devices, extended(): before = lax.ppermute(last, axis, up)  8.51 us
    all_to_all x1, waiting for transfers between devices, shards(): lax.all_to_all(parcel, 'grp', split_axis=1, concat_axis=1, tiled=True)  7.65 us
  transfers between devices with their start and end apart: 26, of which 8 were waited for; matrix products, arithmetic and copies ran while one was open for 9% of the time, Pallas kernels for 0%

commit v1 on v0

--- a/solution.py
+++ b/solution.py
@@ -38,7 +38,7 @@
 
 def by_axis(array, axes):
     for axis in axes:
-        array = lax.psum(array, axis)
+        array = jnp.sum(lax.all_gather(array, axis), axis=0)
     return array
 
 

time: 342 us -> 393 us (1.15)
  local copies, waits for them, and re-layouts: 39.4 us -> 77.4 us
  other arithmetic: 56.2 us -> 75 us
  blocking collectives: 107 us -> 100 us
    psum x12 -> x0, blocking collectives: 107 us -> none  [by_axis(): array = lax.psum(array, axis)]
    unnamed x0 -> x12, blocking collectives: none -> 100 us
    unnamed x81 -> x131, local copies, waits for them, and re-layouts: 12.2 us -> 49.4 us
    reduce_sum x0 -> x24, other arithmetic: none -> 15.3 us  [by_axis(): array = jnp.sum(lax.all_gather(array, axis), axis=0)]
  transfers between devices with their start and end apart: 26 -> 26, of which waited for: 8 -> 9; matrix products, arithmetic and copies ran while one was open for 9% -> 7% of each run, Pallas kernels for 0% -> 0%
where the time goes in v1:
time: 393 us; the launch traced here: 387 us
  blocking collectives  100 us (25%)
  starting transfers between devices  77.8 us (20%)
  local copies, waits for them, and re-layouts  77.4 us (20%)
  other arithmetic  75 us (19%)
  waiting for transfers between devices  44.4 us (11%)
  between operations  11.7 us (3%)
    unnamed x12, blocking collectives  100 us
    unnamed x131, local copies, waits for them, and re-layouts  49.4 us
    ppermute x10, starting transfers between devices, with_halo(): lax.ppermute(last, axis, up)  39.3 us
    all_to_all x1, waiting for transfers between devices, shards(): lax.all_to_all(outgoing, 'grp', split_axis=2, concat_axis=2, tiled=True)  22.3 us
    ppermute x10, starting transfers between devices, with_halo(): lax.ppermute(first, axis, [(b, a) for a, b in up])  18 us
    reduce_sum x24, other arithmetic, by_axis(): array = jnp.sum(lax.all_gather(array, axis), axis=0)  15.3 us
    ppermute x2, starting transfers between devices, extended(): before = lax.ppermute(last, axis, up)  8.52 us
  transfers between devices with their start and end apart: 26, of which 9 were waited for; matrix products, arithmetic and copies ran while one was open for 7% of the time, Pallas kernels for 0%

profile of v1, /device:TPU:1, one launch (start us, length us, event | category | flops | bytes accessed | tf_op | source)
XLA Modules:
  0.0 386.6 jit_solution(14146664448258719174)
XLA Ops:
  3.9 5.1 %all-to-all-start = ((f32[2,2,4,64,512]{4,3,0,1,2:T(8,128)}), f32[2,2,4,64,512]{4,3,0,1,2:T(8,128)}, u32[]{:S(2)}, u32[]{:S(2)}) async-start(f32[2,2,4,64,512]{4,3,0,1,2:T(8,128)} %copy.115), calls=%async_computation | async-start | bytes 4194304 | tf_op jit(solution)/shard_map/all_to_all | solution.py:171
  12.7 22.3 %all-to-all-done = f32[2,2,4,64,512]{4,3,0,1,2:T(8,128)} async-done(((f32[2,2,4,64,512]{4,3,0,1,2:T(8,128)}), f32[2,2,4,64,512]{4,3,0,1,2:T(8,128)}, u32[]{:S(2)}, u32[]{:S(2)}) %all-to-all-start) | async-done | bytes 2097184 | tf_op jit(solution)/shard_map/all_to_all | solution.py:171
  43.7 5.6 %collective-permute-done = f32[12,2,8,512]{3,2,1,0:T(8,128)S(1)} collective-permute-done((f32[12,2,8,512]{3,2,1,0:T(8,128)S(1)}, f32[12,2,8,512]{3,2,1,0:T(8,128)S(1)}, u32[]{:S(2)}, u32[]{:S(2)}) %collective-permute-start) | collective-permute-done | bytes 393248 | tf_op jit(solution)/shard_map/ppermute | solution.py:52
  49.3 3.9 collective-permute-done.1
  57.7 6.1 %collective-permute-start.2 = (f32[12,2,80,8]{2,3,1,0:T(8,128)}, f32[12,2,80,8]{2,3,1,0:T(8,128)}, u32[]{:S(2)}, u32[]{:S(2)}) collective-permute-start(f32[12,2,80,8]{2,3,1,0:T(8,128)} %copy.121), channel_id=1, source_target_pairs={{0,1},{1,2},{2,3},{3,4},{4,5},{5,6},{6,7},{7,8},{8,9},{9,10},{10,1... | collective-permute-start | bytes 184328 | tf_op jit(solution)/shard_map/ppermute | solution.py:52
  74.4 4.6 %pad_maximum_fusion = f32[12,2,80,528]{3,2,1,0:T(8,128)S(1)} fusion(f32[12,2,80,8]{3,2,1,0:T(8,128)} %copy.124, f32[12,2,8,512]{3,2,1,0:T(8,128)} %copy-done.2, f32[12,2,64,512]{3,2,1,0:T(8,128)S(1)} %constant_dynamic-update-slice_fusion, f32[12,2,8,512]{3,2,1,0:T(8,128)S(1)} %collective-permute-done, f32[12,2,80,8]{3,2,1,0:T(8,128)} %copy.123), kind=kLoop, calls=%fused_computation | loop fusion | flops 4055040 | bytes 8110080 | tf_op jit(solution)/shard_map/concatenate | solution.py:54
  112.6 3.6 all-to-all-start.1
  121.7 7.6 %all-to-all-done.1 = f32[2,4,64,512]{3,2,0,1:T(8,128)S(1)} async-done(((f32[2,4,64,512]{3,2,0,1:T(8,128)}), f32[2,4,64,512]{3,2,0,1:T(8,128)S(1)}, u32[]{:S(2)}, u32[]{:S(2)}) %all-to-all-start.1) | async-done | bytes 1048608 | tf_op jit(solution)/shard_map/all_to_all | solution.py:198
  142.0 4.4 %collective-permute-start.5 = (f32[3,256,1]{1,2,0:T(1,128)S(1)}, f32[3,256,1]{1,2,0:T(1,128)S(1)}, u32[]{:S(2)}, u32[]{:S(2)}) collective-permute-start(f32[3,256,1]{1,2,0:T(1,128)S(1)} %get-tuple-element.96), channel_id=1, source_target_pairs={{0,1},{1,2},{2,3},{3,4},{4,5},{5,6},{6,7},{7,8},{8,9},{9,10},{10,1... | collective-permute-start | bytes 9224 | tf_op jit(solution)/shard_map/ppermute | solution.py:27
  151.7 3.6 collective-permute-start.11
  157.9 5.6 %collective-permute-start.9 = (f32[1,512]{0,1:T(8,128)}, f32[1,512]{0,1:T(8,128)}, u32[]{:S(2)}, u32[]{:S(2)}) collective-permute-start(f32[1,512]{0,1:T(8,128)} %copy.149), channel_id=1, source_target_pairs={{0,32},{32,64},{64,96},{1,33},{33,65},{65,97},{2,34},{34,66},{66,9... | collective-permute-start | bytes 6152 | tf_op jit(solution)/shard_map/ppermute | solution.py:27
  168.5 4.1 %fusion.196 = (f32[256,512]{0,1:T(8,128)S(1)}, f32[256,512]{0,1:T(8,128)S(1)}, f32[256,512]{0,1:T(8,128)}, f32[256,512]{0,1:T(8,128)}, f32[256,512]{0,1:T(8,128)}, /*index=5*/f32[256,512]{0,1:T(8,128)}, f32[256,512]{0,1:T(8,128)}) fusion(f32[256,512]{0,1:T(8,128)S(1)} %copy-done.18, f32[1,512]{0,1:T(8,128)} %copy-done.29, ...), kind=kLoop, calls=%fused_computation.471 | loop fusion | flops 6291456 | bytes 11610624 | tf_op jit(solution)/shard_map/div | solution.py:217
  174.7 4.5 %collective-permute-start.13 = (f32[1,512]{0,1:T(8,128)}, f32[1,512]{0,1:T(8,128)S(1)}, u32[]{:S(2)}, u32[]{:S(2)}) collective-permute-start(f32[1,512]{0,1:T(8,128)} %get-tuple-element.165), channel_id=1, source_target_pairs={{0,32},{32,64},{64,96},{1,33},{33,65},{65,97},{2,34},{34,66},{66,9... | collective-permute-start | bytes 6152 | tf_op jit(solution)/shard_map/ppermute | solution.py:27
  181.3 3.7 collective-permute-start.15
  186.6 3.9 %multiply_reduce_fusion.3 = (f32[]{:T(128)}, f32[]{:T(128)}, f32[256,512]{0,1:T(8,128)S(1)}) fusion(f32[256,512]{0,1:T(8,128)} %copy-done.4, f32[256,512]{0,1:T(8,128)S(1)} %get-tuple-element.50, f32[256,512]{0,1:T(8,128)} %get-tuple-element.55, f32[1,512]{0,1:T(8,128)} %copy-done.30, f32[1,512]{0,1:T(8,128)} %copy-done.31, ...), kind=kLoop, calls=%fused_computation.229 | loop fusion | flops 4063230 | bytes 3676168 | tf_op jit(solution)/shard_map/reduce_sum | solution.py:133
  193.8 9.2 %all-reduce.58 = (f32[4]{0:T(128)S(1)}, f32[4]{0:T(128)S(1)}) all-reduce(f32[4]{0:T(128)S(1)} %dynamic-update-slice, f32[4]{0:T(128)S(1)} %dynamic-update-slice.4), channel_id=1, replica_groups=mesh['grp'=4,'tile_0'=4,'tile_1'=4,'tile_2'=2] {'grp'}, use_global_device_ids=true, to_apply=%add.26 | all-reduce | flops 8 | bytes 64
  207.6 9.5 %all-reduce.55 = (f32[4]{0:T(128)S(1)}, f32[4]{0:T(128)S(1)}) all-reduce(f32[4]{0:T(128)S(1)} %dynamic-update-slice.1, f32[4]{0:T(128)S(1)} %dynamic-update-slice.5), channel_id=1, replica_groups=mesh['grp'=4,'tile_0'=4,'tile_1'=4,'tile_2'=2] {'tile_0'}, use_global_device_ids=true, to_apply=%add.27 | all-reduce | flops 8 | bytes 64
  221.6 8.6 %all-reduce.52 = (f32[4]{0:T(128)S(1)}, f32[4]{0:T(128)S(1)}) all-reduce(f32[4]{0:T(128)S(1)} %dynamic-update-slice.2, f32[4]{0:T(128)S(1)} %dynamic-update-slice.6), channel_id=1, replica_groups=mesh['grp'=4,'tile_0'=4,'tile_1'=4,'tile_2'=2] {'tile_1'}, use_global_device_ids=true, to_apply=%add.28 | all-reduce | flops 8 | bytes 64
  234.3 9.7 %all-reduce.61 = (f32[2]{0:T(128)S(1)}, f32[2]{0:T(128)S(1)}) all-reduce(f32[2]{0:T(128)S(1)} %dynamic-update-slice.3, f32[2]{0:T(128)S(1)} %dynamic-update-slice.7), channel_id=1, replica_groups=mesh['grp'=4,'tile_0'=4,'tile_1'=4,'tile_2'=2] {'tile_2'}, use_global_device_ids=true, to_apply=%add.29 | all-reduce | flops 4 | bytes 32
  249.4 4.3 %collective-permute-start.17 = (f32[1,512]{0,1:T(8,128)S(1)}, f32[1,512]{0,1:T(8,128)S(1)}, u32[]{:S(2)}, u32[]{:S(2)}) collective-permute-start(f32[1,512]{0,1:T(8,128)S(1)} %get-tuple-element.161), channel_id=1, source_target_pairs={{0,32},{32,64},{64,96},{1,33},{33,65},{65,97},{2,34},{34,66},{66,9... | collective-permute-start | bytes 6152 | tf_op jit(solution)/shard_map/ppermute | solution.py:27
  253.6 2.8 collective-permute-start.18
  256.4 3.5 collective-permute-start.19
  265.6 6.8 %all-reduce.57 = (f32[4]{0:T(128)S(1)}, f32[4]{0:T(128)S(1)}) all-reduce(f32[4]{0:T(128)S(1)} %dynamic-update-slice.8, f32[4]{0:T(128)S(1)} %dynamic-update-slice.12), channel_id=1, replica_groups=mesh['grp'=4,'tile_0'=4,'tile_1'=4,'tile_2'=2] {'grp'}, use_global_device_ids=true, to_apply=%add.34 | all-reduce | flops 8 | bytes 64
  276.5 6.7 %all-reduce.54 = (f32[4]{0:T(128)S(1)}, f32[4]{0:T(128)S(1)}) all-reduce(f32[4]{0:T(128)S(1)} %dynamic-update-slice.9, f32[4]{0:T(128)S(1)} %dynamic-update-slice.13), channel_id=1, replica_groups=mesh['grp'=4,'tile_0'=4,'tile_1'=4,'tile_2'=2] {'tile_0'}, use_global_device_ids=true, to_apply=%add.35 | all-reduce | flops 8 | bytes 64
  287.1 8.4 %all-reduce.51 = (f32[4]{0:T(128)S(1)}, f32[4]{0:T(128)S(1)}) all-reduce(f32[4]{0:T(128)S(1)} %dynamic-update-slice.10, f32[4]{0:T(128)S(1)} %dynamic-update-slice.14), channel_id=1, replica_groups=mesh['grp'=4,'tile_0'=4,'tile_1'=4,'tile_2'=2] {'tile_1'}, use_global_device_ids=true, to_apply=%add.36 | all-reduce | flops 8 | bytes 64
  299.7 9.9 %all-reduce.60 = (f32[2]{0:T(128)S(1)}, f32[2]{0:T(128)S(1)}) all-reduce(f32[2]{0:T(128)S(1)} %dynamic-update-slice.11, f32[2]{0:T(128)S(1)} %dynamic-update-slice.15), channel_id=1, replica_groups=mesh['grp'=4,'tile_0'=4,'tile_1'=4,'tile_2'=2] {'tile_2'}, use_global_device_ids=true, to_apply=%add.37 | all-reduce | flops 4 | bytes 32
  318.2 4.0 %collective-permute-start.21 = (f32[1,512]{0,1:T(8,128)S(1)}, f32[1,512]{0,1:T(8,128)S(1)}, u32[]{:S(2)}, u32[]{:S(2)}) collective-permute-start(f32[1,512]{0,1:T(8,128)S(1)} %get-tuple-element.157), channel_id=1, source_target_pairs={{0,32},{32,64},{64,96},{1,33},{33,65},{65,97},{2,34},{34,66},{66,9... | collective-permute-start | bytes 6152 | tf_op jit(solution)/shard_map/ppermute | solution.py:27
  325.1 3.5 collective-permute-start.23
  333.4 6.6 %all-reduce.56 = (f32[4]{0:T(128)S(1)}, f32[4]{0:T(128)S(1)}) all-reduce(f32[4]{0:T(128)S(1)} %dynamic-update-slice.16, f32[4]{0:T(128)S(1)} %dynamic-update-slice.20), channel_id=1, replica_groups=mesh['grp'=4,'tile_0'=4,'tile_1'=4,'tile_2'=2] {'grp'}, use_global_device_ids=true, to_apply=%add.42 | all-reduce | flops 8 | bytes 64
  344.0 6.7 %all-reduce.53 = (f32[4]{0:T(128)S(1)}, f32[4]{0:T(128)S(1)}) all-reduce(f32[4]{0:T(128)S(1)} %dynamic-update-slice.17, f32[4]{0:T(128)S(1)} %dynamic-update-slice.21), channel_id=1, replica_groups=mesh['grp'=4,'tile_0'=4,'tile_1'=4,'tile_2'=2] {'tile_0'}, use_global_device_ids=true, to_apply=%add.43 | all-reduce | flops 8 | bytes 64
  355.7 8.3 %all-reduce.50 = (f32[4]{0:T(128)S(1)}, f32[4]{0:T(128)S(1)}) all-reduce(f32[4]{0:T(128)S(1)} %dynamic-update-slice.18, f32[4]{0:T(128)S(1)} %dynamic-update-slice.22), channel_id=1, replica_groups=mesh['grp'=4,'tile_0'=4,'tile_1'=4,'tile_2'=2] {'tile_1'}, use_global_device_ids=true, to_apply=%add.44 | all-reduce | flops 8 | bytes 64
  369.9 10.0 %all-reduce.59 = (f32[2]{0:T(128)S(1)}, f32[2]{0:T(128)S(1)}) all-reduce(f32[2]{0:T(128)S(1)} %dynamic-update-slice.19, f32[2]{0:T(128)S(1)} %dynamic-update-slice.23), channel_id=1, replica_groups=mesh['grp'=4,'tile_0'=4,'tile_1'=4,'tile_2'=2] {'tile_2'}, use_global_device_ids=true, to_apply=%add.45 | all-reduce | flops 4 | bytes 32
  (326 shorter events, 167.8 us)
Async XLA Ops:
  3.9 31.1 %all-to-all-start = ((f32[2,2,4,64,512]{4,3,0,1,2:T(8,128)}), f32[2,2,4,64,512]{4,3,0,1,2:T(8,128)}, u32[]{:S(2)}, u32[]{:S(2)}) async-start(f32[2,2,4,64,512]{4,3,0,1,2:T(8,128)} %copy.115), calls=%async_computation | async-start | bytes 4194304 | tf_op jit(solution)/shard_map/all_to_all | solution.py:171
  9.4 30.4 %copy-start.21 = (f32[2,64,512]{2,1,0:T(8,128)}, f32[2,64,512]{2,1,0:T(8,128)S(1)}, u32[]{:S(2)}) copy-start(f32[2,64,512]{2,1,0:T(8,128)S(1)} %copy.114) | copy-start | bytes 786436
  39.9 9.4 %collective-permute-start = (f32[12,2,8,512]{3,2,1,0:T(8,128)S(1)}, f32[12,2,8,512]{3,2,1,0:T(8,128)S(1)}, u32[]{:S(2)}, u32[]{:S(2)}) collective-permute-start(f32[12,2,8,512]{3,2,1,0:T(8,128)S(1)} %get-tuple-element.93), channel_id=1, source_target_pairs={{0,32},{32,64},{64,96},{1,33},{33,65},{65,97},{2,34},{34,66},{66,9... | collective-permute-start | bytes 1179656 | tf_op jit(solution)/shard_map/ppermute | solution.py:52
  42.4 10.8 %collective-permute-start.1 = (f32[12,2,8,512]{3,2,1,0:T(8,128)S(1)}, f32[12,2,8,512]{3,2,1,0:T(8,128)S(1)}, u32[]{:S(2)}, u32[]{:S(2)}) collective-permute-start(f32[12,2,8,512]{3,2,1,0:T(8,128)S(1)} %get-tuple-element.94), channel_id=1, source_target_pairs={{32,0},{64,32},{96,64},{33,1},{65,33},{97,65},{34,2},{66,34},{98,6... | collective-permute-start | bytes 1179656 | tf_op jit(solution)/shard_map/ppermute | solution.py:53
  57.7 10.2 %collective-permute-start.2 = (f32[12,2,80,8]{2,3,1,0:T(8,128)}, f32[12,2,80,8]{2,3,1,0:T(8,128)}, u32[]{:S(2)}, u32[]{:S(2)}) collective-permute-start(f32[12,2,80,8]{2,3,1,0:T(8,128)} %copy.121), channel_id=1, source_target_pairs={{0,1},{1,2},{2,3},{3,4},{4,5},{5,6},{6,7},{7,8},{8,9},{9,10},{10,1... | collective-permute-start | bytes 184328 | tf_op jit(solution)/shard_map/ppermute | solution.py:52
  65.9 6.2 %collective-permute-start.3 = (f32[12,2,80,8]{2,3,1,0:T(8,128)}, f32[12,2,80,8]{2,3,1,0:T(8,128)}, u32[]{:S(2)}, u32[]{:S(2)}) collective-permute-start(f32[12,2,80,8]{2,3,1,0:T(8,128)} %copy.122), channel_id=1, source_target_pairs={{1,0},{2,1},{3,2},{4,3},{5,4},{6,5},{7,6},{8,7},{9,8},{10,9},{11,1... | collective-permute-start | bytes 184328 | tf_op jit(solution)/shard_map/ppermute | solution.py:53
  112.6 16.7 %all-to-all-start.1 = ((f32[2,4,64,512]{3,2,0,1:T(8,128)}), f32[2,4,64,512]{3,2,0,1:T(8,128)S(1)}, u32[]{:S(2)}, u32[]{:S(2)}) async-start(f32[2,4,64,512]{3,2,0,1:T(8,128)} %pad_maximum_fusion.3), calls=%async_computation.1 | async-start | bytes 2097152 | tf_op jit(solution)/shard_map/all_to_all | solution.py:198
  116.5 49.8 %collective-permute-start.10 = (f32[256,1]{0,1:T(1,128)S(1)}, f32[256,1]{0,1:T(1,128)S(1)}, u32[]{:S(2)}, u32[]{:S(2)}) collective-permute-start(f32[256,1]{0,1:T(1,128)S(1)} %get-tuple-element.169), channel_id=1, source_target_pairs={{1,0},{2,1},{3,2},{4,3},{5,4},{6,5},{7,6},{8,7},{9,8},{10,9},{11,1... | collective-permute-start | bytes 3080 | tf_op jit(solution)/shard_map/ppermute | solution.py:28
  137.1 18.4 %collective-permute-start.4 = (f32[3,1,512]{2,1,0:T(1,128)S(1)}, f32[3,1,512]{2,1,0:T(1,128)S(1)}, u32[]{:S(2)}, u32[]{:S(2)}) collective-permute-start(f32[3,1,512]{2,1,0:T(1,128)S(1)} %copy.139), channel_id=1, source_target_pairs={{0,32},{32,64},{64,96},{1,33},{33,65},{65,97},{2,34},{34,66},{66,9... | collective-permute-start | bytes 18440 | tf_op jit(solution)/shard_map/ppermute | solution.py:27
  140.7 17.3 %collective-permute-start.6 = (f32[3,1,512]{2,1,0:T(1,128)S(1)}, f32[3,1,512]{2,1,0:T(1,128)S(1)}, u32[]{:S(2)}, u32[]{:S(2)}) collective-permute-start(f32[3,1,512]{2,1,0:T(1,128)S(1)} %copy.141), channel_id=1, source_target_pairs={{32,0},{64,32},{96,64},{33,1},{65,33},{97,65},{34,2},{66,34},{98,6... | collective-permute-start | bytes 18440 | tf_op jit(solution)/shard_map/ppermute | solution.py:28
  142.0 9.7 %collective-permute-start.5 = (f32[3,256,1]{1,2,0:T(1,128)S(1)}, f32[3,256,1]{1,2,0:T(1,128)S(1)}, u32[]{:S(2)}, u32[]{:S(2)}) collective-permute-start(f32[3,256,1]{1,2,0:T(1,128)S(1)} %get-tuple-element.96), channel_id=1, source_target_pairs={{0,1},{1,2},{2,3},{3,4},{4,5},{5,6},{6,7},{7,8},{8,9},{9,10},{10,1... | collective-permute-start | bytes 9224 | tf_op jit(solution)/shard_map/ppermute | solution.py:27
  146.3 18.4 %collective-permute-start.7 = (f32[3,256,1]{1,2,0:T(1,128)S(1)}, f32[3,256,1]{1,2,0:T(1,128)S(1)}, u32[]{:S(2)}, u32[]{:S(2)}) collective-permute-start(f32[3,256,1]{1,2,0:T(1,128)S(1)} %get-tuple-element.95), channel_id=1, source_target_pairs={{1,0},{2,1},{3,2},{4,3},{5,4},{6,5},{7,6},{8,7},{9,8},{10,9},{11,1... | collective-permute-start | bytes 9224 | tf_op jit(solution)/shard_map/ppermute | solution.py:28
  151.7 14.6 %collective-permute-start.11 = (f32[256,1]{0,1:T(1,128)S(1)}, f32[256,1]{0,1:T(1,128)S(1)}, u32[]{:S(2)}, u32[]{:S(2)}) collective-permute-start(f32[256,1]{0,1:T(1,128)S(1)} %get-tuple-element.170), channel_id=1, source_target_pairs={{0,1},{1,2},{2,3},{3,4},{4,5},{5,6},{6,7},{7,8},{8,9},{9,10},{10,1... | collective-permute-start | bytes 3080 | tf_op jit(solution)/shard_map/ppermute | solution.py:27
  155.4 10.9 %collective-permute-start.8 = (f32[1,512]{0,1:T(8,128)}, f32[1,512]{0,1:T(8,128)S(1)}, u32[]{:S(2)}, u32[]{:S(2)}) collective-permute-start(f32[1,512]{0,1:T(8,128)} %copy.146), channel_id=1, source_target_pairs={{32,0},{64,32},{96,64},{33,1},{65,33},{97,65},{34,2},{66,34},{98,6... | collective-permute-start | bytes 6152 | tf_op jit(solution)/shard_map/ppermute | solution.py:28
  157.9 10.5 %collective-permute-start.9 = (f32[1,512]{0,1:T(8,128)}, f32[1,512]{0,1:T(8,128)}, u32[]{:S(2)}, u32[]{:S(2)}) collective-permute-start(f32[1,512]{0,1:T(8,128)} %copy.149), channel_id=1, source_target_pairs={{0,32},{32,64},{64,96},{1,33},{33,65},{65,97},{2,34},{34,66},{66,9... | collective-permute-start | bytes 6152 | tf_op jit(solution)/shard_map/ppermute | solution.py:27
  166.3 18.8 %copy-start.37 = (u32[128]{0:T(128)S(1)}, u32[128]{0:T(128)}, u32[]{:S(2)}) copy-start(u32[128]{0:T(128)} %constant.90) | copy-start | bytes 1540
  173.4 12.4 %collective-permute-start.12 = (f32[1,512]{0,1:T(8,128)}, f32[1,512]{0,1:T(8,128)S(1)}, u32[]{:S(2)}, u32[]{:S(2)}) collective-permute-start(f32[1,512]{0,1:T(8,128)} %get-tuple-element.166), channel_id=1, source_target_pairs={{32,0},{64,32},{96,64},{33,1},{65,33},{97,65},{34,2},{66,34},{98,6... | collective-permute-start | bytes 6152 | tf_op jit(solution)/shard_map/ppermute | solution.py:28
  174.7 11.1 %collective-permute-start.13 = (f32[1,512]{0,1:T(8,128)}, f32[1,512]{0,1:T(8,128)S(1)}, u32[]{:S(2)}, u32[]{:S(2)}) collective-permute-start(f32[1,512]{0,1:T(8,128)} %get-tuple-element.165), channel_id=1, source_target_pairs={{0,32},{32,64},{64,96},{1,33},{33,65},{65,97},{2,34},{34,66},{66,9... | collective-permute-start | bytes 6152 | tf_op jit(solution)/shard_map/ppermute | solution.py:27
  179.2 6.5 %collective-permute-start.14 = (f32[256,1]{0,1:T(1,128)S(1)}, f32[256,1]{0,1:T(1,128)S(1)}, u32[]{:S(2)}, u32[]{:S(2)}) collective-permute-start(f32[256,1]{0,1:T(1,128)S(1)} %get-tuple-element.163), channel_id=1, source_target_pairs={{1,0},{2,1},{3,2},{4,3},{5,4},{6,5},{7,6},{8,7},{9,8},{10,9},{11,1... | collective-permute-start | bytes 3080 | tf_op jit(solution)/shard_map/ppermute | solution.py:28
  181.3 4.5 %collective-permute-start.15 = (f32[256,1]{0,1:T(1,128)S(1)}, f32[256,1]{0,1:T(1,128)S(1)}, u32[]{:S(2)}, u32[]{:S(2)}) collective-permute-start(f32[256,1]{0,1:T(1,128)S(1)} %get-tuple-element.164), channel_id=1, source_target_pairs={{0,1},{1,2},{2,3},{3,4},{4,5},{5,6},{6,7},{7,8},{8,9},{9,10},{10,1... | collective-permute-start | bytes 3080 | tf_op jit(solution)/shard_map/ppermute | solution.py:27
  186.6 20.4 %copy-start.35 = (u32[128]{0:T(128)S(1)}, u32[128]{0:T(128)}, u32[]{:S(2)}) copy-start(u32[128]{0:T(128)} %constant.100) | copy-start | bytes 1540
  186.6 34.4 %copy-start.34 = (u32[128]{0:T(128)S(1)}, u32[128]{0:T(128)}, u32[]{:S(2)}) copy-start(u32[128]{0:T(128)} %constant.105) | copy-start | bytes 1540
  248.1 12.6 %collective-permute-start.16 = (f32[1,512]{0,1:T(8,128)S(1)}, f32[1,512]{0,1:T(8,128)S(1)}, u32[]{:S(2)}, u32[]{:S(2)}) collective-permute-start(f32[1,512]{0,1:T(8,128)S(1)} %get-tuple-element.162), channel_id=1, source_target_pairs={{32,0},{64,32},{96,64},{33,1},{65,33},{97,65},{34,2},{66,34},{98,6... | collective-permute-start | bytes 6152 | tf_op jit(solution)/shard_map/ppermute | solution.py:28
  249.4 11.3 %collective-permute-start.17 = (f32[1,512]{0,1:T(8,128)S(1)}, f32[1,512]{0,1:T(8,128)S(1)}, u32[]{:S(2)}, u32[]{:S(2)}) collective-permute-start(f32[1,512]{0,1:T(8,128)S(1)} %get-tuple-element.161), channel_id=1, source_target_pairs={{0,32},{32,64},{64,96},{1,33},{33,65},{65,97},{2,34},{34,66},{66,9... | collective-permute-start | bytes 6152 | tf_op jit(solution)/shard_map/ppermute | solution.py:27
  253.6 6.4 %collective-permute-start.18 = (f32[256,1]{0,1:T(1,128)S(1)}, f32[256,1]{0,1:T(1,128)S(1)}, u32[]{:S(2)}, u32[]{:S(2)}) collective-permute-start(f32[256,1]{0,1:T(1,128)S(1)} %get-tuple-element.159), channel_id=1, source_target_pairs={{1,0},{2,1},{3,2},{4,3},{5,4},{6,5},{7,6},{8,7},{9,8},{10,9},{11,1... | collective-permute-start | bytes 3080 | tf_op jit(solution)/shard_map/ppermute | solution.py:28
  256.4 4.2 %collective-permute-start.19 = (f32[256,1]{0,1:T(1,128)S(1)}, f32[256,1]{0,1:T(1,128)S(1)}, u32[]{:S(2)}, u32[]{:S(2)}) collective-permute-start(f32[256,1]{0,1:T(1,128)S(1)} %get-tuple-element.160), channel_id=1, source_target_pairs={{0,1},{1,2},{2,3},{3,4},{4,5},{5,6},{6,7},{7,8},{8,9},{9,10},{10,1... | collective-permute-start | bytes 3080 | tf_op jit(solution)/shard_map/ppermute | solution.py:27
  316.9 12.4 %collective-permute-start.20 = (f32[1,512]{0,1:T(8,128)S(1)}, f32[1,512]{0,1:T(8,128)S(1)}, u32[]{:S(2)}, u32[]{:S(2)}) collective-permute-start(f32[1,512]{0,1:T(8,128)S(1)} %get-tuple-element.158), channel_id=1, source_target_pairs={{32,0},{64,32},{96,64},{33,1},{65,33},{97,65},{34,2},{66,34},{98,6... | collective-permute-start | bytes 6152 | tf_op jit(solution)/shard_map/ppermute | solution.py:28
  318.2 11.1 %collective-permute-start.21 = (f32[1,512]{0,1:T(8,128)S(1)}, f32[1,512]{0,1:T(8,128)S(1)}, u32[]{:S(2)}, u32[]{:S(2)}) collective-permute-start(f32[1,512]{0,1:T(8,128)S(1)} %get-tuple-element.157), channel_id=1, source_target_pairs={{0,32},{32,64},{64,96},{1,33},{33,65},{65,97},{2,34},{34,66},{66,9... | collective-permute-start | bytes 6152 | tf_op jit(solution)/shard_map/ppermute | solution.py:27
  322.2 6.4 %collective-permute-start.22 = (f32[256,1]{0,1:T(1,128)S(1)}, f32[256,1]{0,1:T(1,128)S(1)}, u32[]{:S(2)}, u32[]{:S(2)}) collective-permute-start(f32[256,1]{0,1:T(1,128)S(1)} %get-tuple-element.155), channel_id=1, source_target_pairs={{1,0},{2,1},{3,2},{4,3},{5,4},{6,5},{7,6},{8,7},{9,8},{10,9},{11,1... | collective-permute-start | bytes 3080 | tf_op jit(solution)/shard_map/ppermute | solution.py:28
  325.1 4.2 %collective-permute-start.23 = (f32[256,1]{0,1:T(1,128)S(1)}, f32[256,1]{0,1:T(1,128)S(1)}, u32[]{:S(2)}, u32[]{:S(2)}) collective-permute-start(f32[256,1]{0,1:T(1,128)S(1)} %get-tuple-element.156), channel_id=1, source_target_pairs={{0,1},{1,2},{2,3},{3,4},{4,5},{5,6},{6,7},{7,8},{8,9},{9,10},{10,1... | collective-permute-start | bytes 3080 | tf_op jit(solution)/shard_map/ppermute | solution.py:27
  340.5 44.6 %copy-start.5 = (f32[256,512]{0,1:T(8,128)S(1)}, f32[256,512]{0,1:T(8,128)}, u32[]{:S(2)}) copy-start(f32[256,512]{0,1:T(8,128)} %copy-done.4) | copy-start | bytes 1572868
  340.5 44.6 %copy-start.19 = (f32[256,512]{0,1:T(8,128)S(1)}, f32[256,512]{0,1:T(8,128)}, u32[]{:S(2)}) copy-start(f32[256,512]{0,1:T(8,128)} %copy-done.17) | copy-start | bytes 1572868
  (32 other events, 214.6 us)
